TPU v7x, 32 devices: a whole 2x2x4 slice. The times are simulated.
32 devices in a mesh: dp: 2 (over x), fsdp: 16 (over z, y, core).
Axes of the slice: x: 2, y: 2, z: 4, core: 2. Of those that a mesh axis runs over, the one named last changes fastest.
Arguments:
- group_grads: bfloat16 [2, 46, 512, 512], P('dp', None, 'fsdp')
- owners: int32 [46, 1], replicated, may hold values from 0 to 15; in each aligned block of 46 rows (0 to 45, 46 to 91, ...) at most 8 rows name the same one
- stats_left: float32 [16, 8, 512, 512], P('fsdp', 'dp'), as said below
- stats_right: float32 [16, 8, 512, 512], P('fsdp', 'dp'), as said below
Outputs:
- preconditioned: bfloat16 [46, 512, 512], P(None, 'fsdp')
Inputs may be any that keep to these rules, and one draw needn't show every extreme that they name: `owners`: no owner names more than 8 blocks, some owner names exactly 8, and every owner 0 to 15 names at least one block. `stats_left`: each [512, 512] matrix is symmetric positive definite. `stats_right`: each [512, 512] matrix is symmetric positive definite.
All inputs are finite; a program needn't handle non-finite values.
Results may differ from a plain program's by a relative error of at most 0.017.
Values may be sent and summed in bfloat16 or wider, within the bound.
A program may use at most 64 MiB of HBM per device.

v0:
```python
import math
import jax
import jax.numpy as jnp
from jax import lax
from jax.experimental import pallas as pl
from jax.experimental.pallas import tpu as pltpu
from jax.sharding import PartitionSpec as P

ITERS = 2


BETA = 0.95

POWER = [math.comb(5, j) * 5.0 ** (5 - j) * (-1.0) ** j / 4.0**6 for j in range(6)]
COEF = [25.0 / 16.0, -5.0 / 16.0 - POWER[0]] + [-POWER[j] for j in range(1, 6)]


def mm(former, latter, dims=((1,), (0,))):
    return lax.dot_general(former, latter, (dims, ((), ())), preferred_element_type=jnp.float32)


def total_of(value):
    return jnp.sum(jnp.sum(value, axis=0, keepdims=True), axis=1, keepdims=True)


def newton_root(statistic):
    magnitude = jnp.sqrt(total_of(statistic * statistic) + 1e-06)
    first = statistic * (1.0 / magnitude)
    low_first = first.astype(jnp.bfloat16)
    second = mm(low_first, low_first)
    third = mm(second.astype(jnp.bfloat16), low_first)
    upper = COEF[4] * first + COEF[5] * second + COEF[6] * third
    lower = COEF[1] * first + COEF[2] * second + COEF[3] * third
    factor = lower + mm(third.astype(jnp.bfloat16), upper.astype(jnp.bfloat16))
    row = lax.broadcasted_iota(jnp.int32, factor.shape, 0)
    column = lax.broadcasted_iota(jnp.int32, factor.shape, 1)
    return (factor + jnp.where(row == column, COEF[0], 0.0)).astype(jnp.bfloat16)


def shape_kernel(gradient_ref, left_ref, right_ref, update_ref):
    gradient = gradient_ref[0]
    left_root = newton_root(BETA * left_ref[0] + mm(gradient, gradient, ((1,), (1,))))
    halfway = mm(left_root, gradient).astype(jnp.bfloat16)
    right_root = newton_root(BETA * right_ref[0] + mm(gradient, gradient, ((0,), (0,))))
    shaped = mm(halfway, right_root)
    wide = gradient.astype(jnp.float32)
    ratio = jnp.sqrt(total_of(wide * wide)) / jnp.sqrt(total_of(shaped * shaped) + 1e-06)
    update_ref[0] = (shaped * ratio).astype(jnp.bfloat16)


def shape_blocks(gradient, left, right, interpret=False):
    count, width, _ = gradient.shape
    spec = pl.BlockSpec((1, width, width), lambda k: (k, 0, 0))
    return pl.pallas_call(
        shape_kernel,
        grid=(count,),
        out_shape=jax.ShapeDtypeStruct(gradient.shape, jnp.bfloat16),
        in_specs=[spec] * 3,
        out_specs=spec,
        compiler_params=pltpu.CompilerParams(vmem_limit_bytes=48 * 1024 * 1024),
        cost_estimate=pl.CostEstimate(
            flops=20 * count * width**3, bytes_accessed=12 * count * width**2, transcendentals=0
        ),
        interpret=interpret,
    )(gradient, left, right)


def shifted(value, groups, step):
    return lax.ppermute(value, "dp", [(g, (g + step) % groups) for g in range(groups)])


def slot_table(owners):
    owner_of = owners[:, 0]
    positions = jnp.arange(owner_of.shape[0], dtype=jnp.int32)
    earlier = (owner_of[None, :] == owner_of[:, None]) & (positions[None, :] < positions[:, None])
    slot_of = jnp.sum(earlier.astype(jnp.int32), axis=1)
    return (owner_of, slot_of, positions)


def body(group_grads, owners, stats_left, stats_right):
    groups = lax.axis_size("dp")
    member = lax.axis_index("dp")
    shards = lax.axis_size("fsdp")
    per_member = stats_left.shape[1]
    capacity = per_member * groups
    owner_of, slot_of, positions = slot_table(owners)
    local = group_grads[0]
    total = local.astype(jnp.float32)
    for step in range(1, groups):
        total = total + shifted(local, groups, step).astype(jnp.float32)
    summed = total.astype(jnp.bfloat16)
    rows_here = summed.shape[1]
    block_width = summed.shape[2]
    wanted = member * per_member + jnp.arange(per_member, dtype=jnp.int32)
    targets = (jnp.arange(shards, dtype=jnp.int32)[:, None] * capacity + wanted[None, :]).reshape(
        -1
    )
    block_key = owner_of * capacity + slot_of
    matches = targets[:, None] == block_key[None, :]
    present = jnp.any(matches, axis=1)
    chosen = jnp.sum(jnp.where(matches, positions[None, :], 0), axis=1)
    outgoing = jnp.where(
        present[:, None, None], jnp.take(summed, chosen, axis=0), jnp.zeros((), jnp.bfloat16)
    )
    outgoing = outgoing.reshape(shards, per_member, rows_here, block_width)
    arrived = lax.all_to_all(outgoing, "fsdp", split_axis=0, concat_axis=2, tiled=True)
    gradient = arrived.reshape(per_member, block_width, block_width)
    update = shape_blocks(gradient, stats_left[0], stats_right[0])
    pieces = update.reshape(per_member, shards, rows_here, block_width)
    returned = lax.all_to_all(pieces, "fsdp", split_axis=1, concat_axis=0, tiled=True)
    returned = returned.reshape(shards * per_member, rows_here, block_width)
    mine = jnp.take(returned, owner_of * per_member + slot_of % per_member, axis=0)
    holder = slot_of // per_member
    result = mine
    for step in range(1, groups):
        theirs = (holder == (member - step) % groups)[:, None, None]
        result = jnp.where(theirs, shifted(mine, groups, step), result)
    return result


def solution(mesh):
    placed = (
        P("dp", None, "fsdp", None),
        P(),
        P("fsdp", "dp", None, None),
        P("fsdp", "dp", None, None),
    )
    return jax.shard_map(
        body, mesh=mesh, in_specs=placed, out_specs=P(None, "fsdp", None), check_vma=False
    )
```

profile of v0, /device:TPU:22, one launch (start us, length us, event | category | flops | bytes accessed | tf_op | source)
XLA Modules:
  0.0 206.6 jit_solution(10242399137706440773)
XLA Ops:
  0.0 0.5 collective-permute-start
  0.5 0.1 broadcast_add_fusion
  0.6 0.1 add.111
  0.7 0.9 convert_reduce_fusion
  1.6 0.7 multiply_add_fusion
  2.3 0.1 compare_reduce_fusion
  2.4 0.1 broadcast_in_dim.64
  2.5 0.1 fusion
  2.6 0.1 reduce_sum.27
  2.7 32.2 %collective-permute-done = bf16[46,32,512]{2,1,0:T(8,128)(2,1)S(1)} collective-permute-done((bf16[46,32,512]{2,1,0:T(8,128)(2,1)}, bf16[46,32,512]{2,1,0:T(8,128)(2,1)S(1)}, u32[]{:S(2)}, u32[]{:S(2)}) %collective-permute-start) | collective-permute-done | bytes 1507360 | tf_op jit(solution)/shard_map/ppermute | solution.py:69
  34.9 1.9 add_convert_fusion
  36.9 2.0 gather_fusion
  38.9 1.9 select_select_fusion
  40.8 51.6 %all_to_all.30 = bf16[16,4,32,512]{3,2,1,0:T(8,128)(2,1)S(1)} all-to-all(bf16[16,4,32,512]{3,2,1,0:T(8,128)(2,1)S(1)} %select_select_fusion), channel_id=1, replica_groups=mesh['dp'=2,'fsdp'=16] {'fsdp'}, dimensions={0} | all-to-all | bytes 4194304 | tf_op jit(solution)/shard_map/all_to_all | solution.py:106
  92.4 0.2 copy.14
  92.7 18.7 %shard_map.46 = bf16[4,512,512]{2,1,0:T(8,128)(2,1)S(1)} custom-call(bf16[4,512,512]{2,1,0:T(8,128)(2,1)S(1)} %bitcast.29, f32[4,512,512]{2,1,0:T(8,128)} %bitcast.37, f32[4,512,512]{2,1,0:T(8,128)} %bitcast.38), custom_call_target="tpu_custom_call" | custom-call | flops 10737418240 | bytes 12582912 | tf_op jit(solution)/shard_map/pallas_call | solution.py:54
  111.4 1.6 copy.15
  113.0 0.0 copy-start.1
  113.0 6.8 %all-to-all-start.1 = ((bf16[4,16,32,512]{3,2,0,1:T(8,128)(2,1)}), bf16[4,16,32,512]{3,2,0,1:T(8,128)(2,1)S(1)}, u32[]{:S(2)}, u32[]{:S(2)}) async-start(bf16[4,16,32,512]{3,2,0,1:T(8,128)(2,1)} %copy.15), calls=%async_computation.1 | async-start | bytes 4194304 | tf_op jit(solution)/shard_map/all_to_all | solution.py:110
  119.8 0.0 copy-done.1
  119.8 45.9 %all-to-all-done.1 = bf16[4,16,32,512]{3,2,0,1:T(8,128)(2,1)S(1)} async-done(((bf16[4,16,32,512]{3,2,0,1:T(8,128)(2,1)}), bf16[4,16,32,512]{3,2,0,1:T(8,128)(2,1)S(1)}, u32[]{:S(2)}, u32[]{:S(2)}) %all-to-all-start.1) | async-done | bytes 2097184 | tf_op jit(solution)/shard_map/all_to_all | solution.py:110
  165.7 0.0 copy-start
  165.7 1.3 copy-done
  167.0 2.2 %gather_fusion.1 = bf16[46,32,512]{2,1,0:T(8,128)(2,1)S(1)} fusion(bf16[64,32,512]{2,1,0:T(8,128)(2,1)} %bitcast.33, s32[1024]{0:T(1024)S(1)} %pad_clamp_fusion), kind=kCustom, calls=%fused_computation.1 | custom fusion | bytes 3014840 | tf_op jit(solution)/shard_map/jit(_take)/gather | solution.py:112
  169.3 1.3 broadcast_select_fusion
  170.6 0.5 collective-permute-start.1
  171.1 34.1 %collective-permute-done.1 = bf16[46,32,512]{2,1,0:T(8,128)(2,1)S(1)} collective-permute-done((bf16[46,32,512]{2,1,0:T(8,128)(2,1)}, bf16[46,32,512]{2,1,0:T(8,128)(2,1)S(1)}, u32[]{:S(2)}, u32[]{:S(2)}) %collective-permute-start.1) | collective-permute-done | bytes 1507360 | tf_op jit(solution)/shard_map/ppermute | solution.py:69
  205.2 1.4 broadcast_select_fusion.1
  (8 shorter events, 0.1 us)
Async XLA Ops:
  0.0 34.9 %collective-permute-start = (bf16[46,32,512]{2,1,0:T(8,128)(2,1)}, bf16[46,32,512]{2,1,0:T(8,128)(2,1)S(1)}, u32[]{:S(2)}, u32[]{:S(2)}) collective-permute-start(bf16[46,32,512]{2,1,0:T(8,128)(2,1)} %bitcast.34), channel_id=1, source_target_pairs={{0,16},{16,0},{1,17},{17,1},{2,18},{18,2},{3,19},{19,3},{4,20},{20... | collective-permute-start | bytes 4521992 | tf_op jit(solution)/shard_map/ppermute | solution.py:69
  113.0 6.8 %copy-start.1 = (s32[46,1]{0,1:T(1,128)S(1)}, s32[46,1]{0,1:T(1,128)}, u32[]{:S(2)}) copy-start(s32[46,1]{0,1:T(1,128)} %param.5) | copy-start | bytes 556
  113.0 52.7 %all-to-all-start.1 = ((bf16[4,16,32,512]{3,2,0,1:T(8,128)(2,1)}), bf16[4,16,32,512]{3,2,0,1:T(8,128)(2,1)S(1)}, u32[]{:S(2)}, u32[]{:S(2)}) async-start(bf16[4,16,32,512]{3,2,0,1:T(8,128)(2,1)} %copy.15), calls=%async_computation.1 | async-start | bytes 4194304 | tf_op jit(solution)/shard_map/all_to_all | solution.py:110
  165.7 1.4 copy-start
  170.6 34.6 %collective-permute-start.1 = (bf16[46,32,512]{2,1,0:T(8,128)(2,1)}, bf16[46,32,512]{2,1,0:T(8,128)(2,1)S(1)}, u32[]{:S(2)}, u32[]{:S(2)}) collective-permute-start(bf16[46,32,512]{2,1,0:T(8,128)(2,1)} %broadcast_select_fusion), channel_id=1, source_target_pairs={{0,16},{16,0},{1,17},{17,1},{2,18},{18,2},{3,19},{19,3},{4,20},{20... | collective-permute-start | bytes 4521992 | tf_op jit(solution)/shard_map/ppermute | solution.py:69
where the time goes:
time: 209 us; the launch traced here: 207 us
  waiting for transfers between devices  112 us (54%)
  blocking collectives  51.6 us (25%)
  Pallas kernels  18.7 us (9%)
  other arithmetic  8.49 us (4%)
  starting transfers between devices  7.86 us (4%)
  local copies, waits for them, and re-layouts  7.73 us (4%)
    ppermute x2, waiting for transfers between devices, shifted(): lax.ppermute(value, 'dp', [(g, (g + step) % groups) for g in range(groups)])  66.3 us
    all_to_all x1, blocking collectives, body(): lax.all_to_all(outgoing, 'fsdp', split_axis=0, concat_axis=2, tiled=True)  51.6 us
    all_to_all x1, waiting for transfers between devices, body(): lax.all_to_all(pieces, 'fsdp', split_axis=1, concat_axis=0, tiled=True)  45.9 us
    pallas_call x1, Pallas kernels, shape_blocks(): pl.pallas_call(shape_kernel, grid=(count,), out_shape=jax.ShapeDtypeStruc...  18.7 us
    all_to_all x1, starting transfers between devices, body(): lax.all_to_all(pieces, 'fsdp', split_axis=1, concat_axis=0, tiled=True)  6.79 us
  transfers between devices with their start and end apart: 3, of which 3 were waited for; matrix products, arithmetic and copies ran while one was open for 1% of the time, Pallas kernels for 0%

commit v1 on v0

--- a/solution.py
+++ b/solution.py
@@ -1,3 +1,4 @@
+import functools
 import math
 import jax
 import jax.numpy as jnp
@@ -75,6 +76,304 @@
     earlier = (owner_of[None, :] == owner_of[:, None]) & (positions[None, :] < positions[:, None])
     slot_of = jnp.sum(earlier.astype(jnp.int32), axis=1)
     return (owner_of, slot_of, positions)
+
+MESH = pl.DeviceIdType.MESH
+
+
+def shape_block(gradient, left, right):
+    left_root = newton_root(BETA * left + mm(gradient, gradient, ((1,), (1,))))
+    halfway = mm(left_root, gradient).astype(jnp.bfloat16)
+    right_root = newton_root(BETA * right + mm(gradient, gradient, ((0,), (0,))))
+    shaped = mm(halfway, right_root)
+    wide = gradient.astype(jnp.float32)
+    ratio = jnp.sqrt(total_of(wide * wide)) / jnp.sqrt(total_of(shaped * shaped) + 1e-06)
+    return (shaped * ratio).astype(jnp.bfloat16)
+
+
+def level_caps(blocks, shards, capacity, levels):
+    caps = [shards]
+    for slot in range(1, levels):
+        caps.append(min(shards, (blocks - capacity + slot + 1 - shards) // slot))
+    return caps
+
+
+def fused_kernel(
+    caps,
+    send_block,
+    own_block,
+    own_rank,
+    pack_owner,
+    pick,
+    grads,
+    left_hbm,
+    right_hbm,
+    out,
+    left,
+    right,
+    x_out,
+    summed,
+    gradient,
+    update,
+    settled,
+    back_out,
+    stat_sem,
+    x_send,
+    x_recv,
+    in_send,
+    in_recv,
+    out_send,
+    out_recv,
+    back_send,
+    back_recv,
+    *landing,
+):
+    levels = len(caps)
+    x_in, result = landing[:levels], landing[levels:]
+    starts = [sum(caps[:s]) for s in range(levels)]
+    shards, rows, width = gradient.shape[1:]
+    group, me = lax.axis_index("dp"), lax.axis_index("fsdp")
+    partner = (1 - group, me)
+
+    def stat_copies(s):
+        return [
+            pltpu.make_async_copy(left_hbm.at[s], left.at[s], stat_sem.at[0, s]),
+            pltpu.make_async_copy(right_hbm.at[s], right.at[s], stat_sem.at[1, s]),
+        ]
+
+    for s in range(levels):
+        for copy in stat_copies(s):
+            copy.start()
+
+    barrier = pltpu.get_barrier_semaphore()
+    pl.semaphore_signal(barrier, inc=1, device_id=partner, device_id_type=MESH)
+
+    @pl.loop(1, shards)
+    def _(k):
+        pl.semaphore_signal(
+            barrier, inc=1, device_id=(group, lax.rem(me + k, shards)), device_id_type=MESH
+        )
+
+    def x_copy(s):
+        part = pl.ds(starts[s], caps[s])
+        return pltpu.make_async_remote_copy(
+            src_ref=x_out.at[part],
+            dst_ref=x_in[s],
+            send_sem=x_send.at[s],
+            recv_sem=x_recv.at[s],
+            device_id=partner,
+            device_id_type=MESH,
+        )
+
+    def fill(s):
+        for i in range(caps[s]):
+            x_out[starts[s] + i] = grads[send_block[s, i]]
+
+    fill(0)
+    pl.semaphore_wait(barrier, shards)
+    x_copy(0).start()
+    for s in range(1, levels):
+        fill(s)
+        x_copy(s).start()
+
+    def in_copy(s, k):
+        owner = lax.rem(me + k, shards)
+        return pltpu.make_async_remote_copy(
+            src_ref=summed.at[s, owner],
+            dst_ref=gradient.at[s, me],
+            send_sem=in_send.at[s, k],
+            recv_sem=in_recv.at[s, k],
+            device_id=(group, owner),
+            device_id_type=MESH,
+        )
+
+    def out_copy(s, k):
+        shard = lax.rem(me + k, shards)
+        return pltpu.make_async_remote_copy(
+            src_ref=update.at[s, shard],
+            dst_ref=result[s].at[me],
+            send_sem=out_send.at[s, k],
+            recv_sem=out_recv.at[s, k],
+            device_id=(group, shard),
+            device_id_type=MESH,
+        )
+
+    def back_copy(s):
+        part = pl.ds(starts[s], caps[s])
+        return pltpu.make_async_remote_copy(
+            src_ref=back_out.at[part],
+            dst_ref=settled.at[pl.ds(levels * shards + starts[s], caps[s])],
+            send_sem=back_send.at[s],
+            recv_sem=back_recv.at[s],
+            device_id=partner,
+            device_id_type=MESH,
+        )
+
+    def scatter(s):
+        x_copy(s).wait_recv()
+
+        @pl.loop(0, shards)
+        def _(o):
+            mine = grads[own_block[s, o]].astype(jnp.float32)
+            theirs = x_in[s][own_rank[s, o]].astype(jnp.float32)
+            summed[s, o] = (mine + theirs).astype(jnp.bfloat16)
+
+        gradient[s, me] = summed[s, me]
+
+        @pl.loop(1, shards)
+        def _(k):
+            in_copy(s, k).start()
+
+    def compute(s):
+        @pl.loop(1, shards)
+        def _(k):
+            in_copy(s, k).wait_recv()
+
+        for copy in stat_copies(s):
+            copy.wait()
+        block = gradient[s].reshape(shards * rows, width)
+        update[s] = shape_block(block, left[s], right[s]).reshape(shards, rows, width)
+
+    def spread(s):
+        result[s][me] = update[s, me]
+
+        @pl.loop(1, shards)
+        def _(k):
+            out_copy(s, k).start()
+
+    def give_back(s):
+        @pl.loop(1, shards)
+        def _(k):
+            out_copy(s, k).wait_recv()
+
+        for i in range(caps[s]):
+            back_out[starts[s] + i] = result[s][pack_owner[s, i]]
+        back_copy(s).start()
+        for o in range(shards):
+            settled[s * shards + o] = result[s][o]
+
+    ahead = min(2, levels)
+    for s in range(ahead):
+        scatter(s)
+
+    @pl.loop(0, levels)
+    def _(step):
+        compute(step)
+        for s in range(levels):
+
+            @pl.when(step == s)
+            def _():
+                spread(s)
+
+        for s in range(ahead, levels):
+
+            @pl.when(step == s - ahead)
+            def _():
+                scatter(s)
+
+        for s in range(levels - 1):
+
+            @pl.when(step == s + 1)
+            def _():
+                give_back(s)
+
+    give_back(levels - 1)
+    for s in range(levels):
+        back_copy(s).wait_recv()
+    for b in range(out.shape[0]):
+        out[b] = settled[pick[b]]
+    for s in range(levels):
+
+        @pl.loop(1, shards)
+        def _(k):
+            in_copy(s, k).wait_send()
+            out_copy(s, k).wait_send()
+
+        x_copy(s).wait_send()
+        back_copy(s).wait_send()
+
+
+def pair_tables(owners, member, shards, levels, caps):
+    owner_of, slot_of, positions = slot_table(owners)
+    slots = jnp.arange(2 * levels, dtype=jnp.int32)
+    names = jnp.arange(shards, dtype=jnp.int32)
+    matches = (slot_of[None, None, :] == slots[:, None, None]) & (
+        owner_of[None, None, :] == names[None, :, None]
+    )
+    block = jnp.sum(jnp.where(matches, positions, 0), axis=2)
+    count = jnp.sum((owner_of[None, :] == names[:, None]).astype(jnp.int32), axis=1)
+    present = count[None, :] > slots[:, None]
+    before = names[None, :] < names[:, None]
+    rank = jnp.sum((present[:, None, :] & before[None]).astype(jnp.int32), axis=2)
+    rank = jnp.where(present, rank, 0)
+    places = jnp.arange(max(caps), dtype=jnp.int32)
+    at_place = present[:, None, :] & (rank[:, None, :] == places[None, :, None])
+    place_block = jnp.sum(jnp.where(at_place, block[:, None, :], 0), axis=2)
+    place_owner = jnp.sum(jnp.where(at_place, names, 0), axis=2)
+
+    def side(table, which):
+        return lax.dynamic_slice_in_dim(table, which * levels, levels, 0)
+
+    level = slot_of % levels
+    start = sum(jnp.where(level > s, caps[s], 0) for s in range(levels))
+    ahead_of = (count[None, :] > slot_of[:, None]) & (names[None, :] < owner_of[:, None])
+    block_rank = jnp.sum(ahead_of.astype(jnp.int32), axis=1)
+    pick = jnp.where(
+        slot_of // levels == member,
+        level * shards + owner_of,
+        levels * shards + start + block_rank,
+    )
+    return (
+        side(place_block, 1 - member),
+        side(block, member),
+        side(rank, member),
+        side(place_owner, member),
+        pick,
+    )
+
+
+def pair_body(group_grads, owners, stats_left, stats_right):
+    shards = lax.axis_size("fsdp")
+    member = lax.axis_index("dp")
+    _, blocks, rows, width = group_grads.shape
+    levels = stats_left.shape[1]
+    caps = level_caps(blocks, shards, 2 * levels, levels)
+    tables = pair_tables(owners, member, shards, levels, caps)
+    piece = (rows, width)
+    dma = pltpu.SemaphoreType.DMA
+    bf16 = jnp.bfloat16
+    vmem = pl.BlockSpec(memory_space=pltpu.VMEM)
+    smem = pl.BlockSpec(memory_space=pltpu.SMEM)
+    anywhere = pl.BlockSpec(memory_space=pl.ANY)
+    return pl.pallas_call(
+        functools.partial(fused_kernel, caps),
+        out_shape=jax.ShapeDtypeStruct((blocks, *piece), bf16),
+        in_specs=[smem] * 5 + [vmem, anywhere, anywhere],
+        out_specs=vmem,
+        scratch_shapes=[
+            pltpu.VMEM((levels, width, width), jnp.float32),
+            pltpu.VMEM((levels, width, width), jnp.float32),
+            pltpu.VMEM((sum(caps), *piece), bf16),
+            pltpu.VMEM((levels, shards, *piece), bf16),
+            pltpu.VMEM((levels, shards, *piece), bf16),
+            pltpu.VMEM((levels, shards, *piece), bf16),
+            pltpu.VMEM((levels * shards + sum(caps), *piece), bf16),
+            pltpu.VMEM((sum(caps), *piece), bf16),
+            dma((2, levels)),
+            dma((levels,)),
+            dma((levels,)),
+            dma((levels, shards)),
+            dma((levels, shards)),
+            dma((levels, shards)),
+            dma((levels, shards)),
+            dma((levels,)),
+            dma((levels,)),
+        ]
+        + [pltpu.VMEM((cap, *piece), bf16) for cap in caps]
+        + [pltpu.VMEM((shards, *piece), bf16)] * levels,
+        compiler_params=pltpu.CompilerParams(
+            collective_id=0, has_side_effects=True, vmem_limit_bytes=56 * 1024 * 1024
+        ),
+    )(*tables, group_grads[0], stats_left[0], stats_right[0])
 
 
 def body(group_grads, owners, stats_left, stats_right):
@@ -126,5 +425,5 @@
         P("fsdp", "dp", None, None),
     )
     return jax.shard_map(
-        body, mesh=mesh, in_specs=placed, out_specs=P(None, "fsdp", None), check_vma=False
-    )
+        pair_body if mesh.shape["dp"] == 2 else body, mesh=mesh, in_specs=placed, out_specs=P(None, "fsdp", None), check_vma=False
+    )

time: 209 us -> 135 us (0.65); the launches traced: 207 us -> 135 us
  waiting for transfers between devices: 112 us -> 0 us
  Pallas kernels: 18.7 us -> 126 us
  blocking collectives: 51.6 us -> 0 us
  starting transfers between devices: 7.86 us -> 0 us
  local copies, waits for them, and re-layouts: 7.73 us -> 3.86 us
  other arithmetic: 8.49 us -> 5.07 us
    pallas_call x1, Pallas kernels: 18.7 us -> 126 us  [pair_body(): pl.pallas_call(functools.partial(fused_kernel, caps), out_shape=jax.Shape...]
    ppermute x2 -> x0, waiting for transfers between devices: 66.3 us -> none  [shifted(): lax.ppermute(value, 'dp', [(g, (g + step) % groups) for g in range(groups)])]
    all_to_all x1 -> x0, blocking collectives: 51.6 us -> none  [body(): lax.all_to_all(outgoing, 'fsdp', split_axis=0, concat_axis=2, tiled=True)]
    all_to_all x1 -> x0, waiting for transfers between devices: 45.9 us -> none  [body(): lax.all_to_all(pieces, 'fsdp', split_axis=1, concat_axis=0, tiled=True)]
    all_to_all x1 -> x0, starting transfers between devices: 6.79 us -> none  [body(): lax.all_to_all(pieces, 'fsdp', split_axis=1, concat_axis=0, tiled=True)]
    gather x2 -> x0, local copies, waits for them, and re-layouts: 4.28 us -> none  [the longest x1 2.24 us: body(): jnp.take(returned, owner_of * per_member + slot_of % per_member, axis=0)]
    select_n x4 -> x2, other arithmetic: 4.65 us -> 1.18 us  [the longest x1 1.17 us: pair_tables(): jnp.where(slot_of // levels == member, level * shards + owner_of, levels...]
    reduce_sum x1 -> x5, other arithmetic: 0.09 us -> 2.3 us  [the longest x1 0.77 us: pair_tables(): jnp.sum((owner_of[None, :] == names[:, None]).astype(jnp.int32), axis=1)]
  transfers between devices with their start and end apart: 3 -> 0, of which waited for: 3 -> 0; matrix products, arithmetic and copies ran while one was open for 1% -> 0% of each run, Pallas kernels for 0% -> 0%
where the time goes in v1:
time: 135 us
  Pallas kernels  126 us (93%)
  other arithmetic  5.07 us (4%)
  local copies, waits for them, and re-layouts  3.86 us (3%)
    pallas_call x1, Pallas kernels, pair_body(): pl.pallas_call(functools.partial(fused_kernel, caps), out_shape=jax.Shape...  126 us

profile of v1, /device:TPU:22, one launch (start us, length us, event | category | flops | bytes accessed | tf_op | source)
XLA Modules:
  0.0 135.2 jit_solution(7588976393435097817)
XLA Ops:
  0.0 0.8 convert_reduce_fusion.3
  0.8 0.9 convert_reduce_fusion.1
  1.7 0.8 convert_reduce_fusion.2
  2.4 1.2 compare_select_fusion.4.pick
  3.6 0.7 iota_compare_fusion.4
  4.3 0.2 select_reduce_fusion.2
  4.5 0.2 convert_reduce_fusion
  4.8 0.6 constant_dynamic-slice_fusion.1
  5.3 0.3 select_reduce_fusion
  5.7 0.6 constant_dynamic-slice_fusion
  6.3 126.2 %shard_map.46 = bf16[46,32,512]{2,1,0:T(8,128)(2,1)} custom-call(s32[4,16]{1,0:T(4,128)} %get-tuple-element.8.send_block, s32[4,16]{1,0:T(4,128)} %get-tuple-element.10.own_block, s32[4,16]{1,0:T(4,128)} %get-tuple-element.9.own_rank, s32[4,16]{1,0:T(4,128)} %get-tuple-element.7.pack_owner, s32[46]{0:T(128)} %compare_select_fusion.4.pick, ...), custom_call_target="tpu_custom_call" | custom-call | tf_op jit(solution)/shard_map/pallas_call | solution.py:347
  132.5 2.7 %copy.6 = bf16[46,32,512]{2,1,0:T(8,128)(2,1)} copy(bf16[46,32,512]{2,1,0:T(8,128)(2,1)} %shard_map.46) | data formatting | bytes 3014656
  (4 shorter events, 0.0 us)

commit v2 on v1

--- a/solution.py
+++ b/solution.py
@@ -11,6 +11,7 @@
 
 
 BETA = 0.95
+AHEAD = 3
 
 POWER = [math.comb(5, j) * 5.0 ** (5 - j) * (-1.0) ** j / 4.0**6 for j in range(6)]
 COEF = [25.0 / 16.0, -5.0 / 16.0 - POWER[0]] + [-POWER[j] for j in range(1, 6)]
@@ -97,24 +98,82 @@
     return caps
 
 
+def visit_order(shards):
+    stride = next(s for s in range(math.isqrt(shards), 0, -1) if shards % s == 0)
+    return stride, [o for r in range(stride) for o in range(r, shards, stride)]
+
+
+def table_kernel(levels, shards, caps, owners_ref, table_ref):
+    blocks = owners_ref.shape[1]
+    stride, _ = visit_order(shards)
+
+    def numbers(shape, axis):
+        return lax.broadcasted_iota(jnp.int32, shape, axis).astype(jnp.float32)
+
+    def split(value, size):
+        quotient = jnp.floor((value + 0.5) * (1.0 / size))
+        return quotient, value - size * quotient
+
+    def visit(owner):
+        quotient, rest = split(owner, stride)
+        return rest * (shards // stride) + quotient
+
+    def down(mask, value=1.0):
+        return jnp.sum(jnp.where(mask, value, 0.0), axis=0, keepdims=True)
+
+    def across(mask, value=1.0):
+        return jnp.sum(jnp.where(mask, value, 0.0), axis=1, keepdims=True)
+
+    square = (blocks, blocks)
+    first, second = numbers(square, 0), numbers(square, 1)
+    owner_row = owners_ref[...].astype(jnp.float32)
+    owner_col = across(first == second, owner_row)
+    same = owner_col == owner_row
+    slot_row = down(same & (first < second))
+    slot_col = across(same & (second < first))
+    visit_row, visit_col = visit(owner_row), visit(owner_col)
+    level = slot_col == slot_row
+    rank_row = down(level & (visit_col < visit_row))
+    rank_col = across(level & (visit_row < visit_col))
+    wide = (blocks, 2 * levels * shards)
+    slot, place = split(numbers(wide, 1), shards)
+    at_owner = (slot_col == slot) & (owner_col == place)
+    at_place = (slot_col == slot) & (rank_col == place)
+    block_col = numbers(wide, 0)
+    rows = [
+        down(at_owner, block_col),
+        down(at_owner, rank_col),
+        down(at_place, block_col),
+        down(at_place, owner_col),
+    ]
+    for r, row in enumerate(rows):
+        table_ref[r : r + 1, 0 : wide[1]] = row.astype(jnp.int32)
+    holder, depth = split(slot_row, levels)
+    start = sum(jnp.where(depth > s, float(caps[s]), 0.0) for s in range(levels))
+    place_row = rank_row
+    for s in range(levels):
+        if caps[s] == shards:
+            place_row = jnp.where(depth == s, owner_row, place_row)
+    for member in range(2):
+        pick = jnp.where(
+            holder == member, depth * shards + owner_row, levels * shards + start + place_row
+        )
+        table_ref[4 + member : 5 + member, 0:blocks] = pick.astype(jnp.int32)
+
+
 def fused_kernel(
     caps,
-    send_block,
-    own_block,
-    own_rank,
-    pack_owner,
-    pick,
+    table,
     grads,
     left_hbm,
     right_hbm,
-    out,
+    settled,
     left,
     right,
     x_out,
     summed,
     gradient,
     update,
-    settled,
     back_out,
     stat_sem,
     x_send,
@@ -128,11 +187,19 @@
     *landing,
 ):
     levels = len(caps)
-    x_in, result = landing[:levels], landing[levels:]
+    x_in, result, back_in = landing[:levels], landing[levels : 2 * levels], landing[2 * levels]
     starts = [sum(caps[:s]) for s in range(levels)]
     shards, rows, width = gradient.shape[1:]
+    full = [cap == shards for cap in caps]
+    stride, order = visit_order(shards)
+    part = shards // stride
+    parts = [(0, i, part) for i in range(0, shards, part)]
+    parts += [(s, 0, caps[s]) for s in range(1, levels)]
     group, me = lax.axis_index("dp"), lax.axis_index("fsdp")
     partner = (1 - group, me)
+
+    def lookup(row, side, s, i):
+        return table[row, (side * levels + s) * shards + i]
 
     def stat_copies(s):
         return [
@@ -140,10 +207,6 @@
             pltpu.make_async_copy(right_hbm.at[s], right.at[s], stat_sem.at[1, s]),
         ]
 
-    for s in range(levels):
-        for copy in stat_copies(s):
-            copy.start()
-
     barrier = pltpu.get_barrier_semaphore()
     pl.semaphore_signal(barrier, inc=1, device_id=partner, device_id_type=MESH)
 
@@ -153,46 +216,50 @@
             barrier, inc=1, device_id=(group, lax.rem(me + k, shards)), device_id_type=MESH
         )
 
-    def x_copy(s):
-        part = pl.ds(starts[s], caps[s])
+    for s in range(levels):
+        for copy in stat_copies(s):
+            copy.start()
+
+    def x_copy(n):
+        s, i, size = parts[n]
         return pltpu.make_async_remote_copy(
-            src_ref=x_out.at[part],
-            dst_ref=x_in[s],
-            send_sem=x_send.at[s],
-            recv_sem=x_recv.at[s],
+            src_ref=x_out.at[pl.ds(starts[s] + i, size)],
+            dst_ref=x_in[s].at[pl.ds(i, size)],
+            send_sem=x_send.at[n],
+            recv_sem=x_recv.at[n],
             device_id=partner,
             device_id_type=MESH,
         )
 
-    def fill(s):
-        for i in range(caps[s]):
-            x_out[starts[s] + i] = grads[send_block[s, i]]
+    def fill(n):
+        s, first, size = parts[n]
+        for i in range(first, first + size):
+            block = lookup(0, 1 - group, s, order[i]) if full[s] else lookup(2, 1 - group, s, i)
+            x_out[starts[s] + i] = grads[block]
 
     fill(0)
     pl.semaphore_wait(barrier, shards)
-    x_copy(0).start()
-    for s in range(1, levels):
-        fill(s)
-        x_copy(s).start()
-
-    def in_copy(s, k):
-        owner = lax.rem(me + k, shards)
+    for n in range(len(parts)):
+        x_copy(n).start()
+        if n + 1 < len(parts):
+            fill(n + 1)
+
+    def in_copy(s, owner, source):
         return pltpu.make_async_remote_copy(
             src_ref=summed.at[s, owner],
-            dst_ref=gradient.at[s, me],
-            send_sem=in_send.at[s, k],
-            recv_sem=in_recv.at[s, k],
+            dst_ref=gradient.at[s, source],
+            send_sem=in_send.at[s, owner],
+            recv_sem=in_recv.at[s, source],
             device_id=(group, owner),
             device_id_type=MESH,
         )
 
-    def out_copy(s, k):
-        shard = lax.rem(me + k, shards)
+    def out_copy(s, shard, source):
         return pltpu.make_async_remote_copy(
             src_ref=update.at[s, shard],
-            dst_ref=result[s].at[me],
-            send_sem=out_send.at[s, k],
-            recv_sem=out_recv.at[s, k],
+            dst_ref=result[s].at[source],
+            send_sem=out_send.at[s, shard],
+            recv_sem=out_recv.at[s, source],
             device_id=(group, shard),
             device_id_type=MESH,
         )
@@ -200,33 +267,58 @@
     def back_copy(s):
         part = pl.ds(starts[s], caps[s])
         return pltpu.make_async_remote_copy(
-            src_ref=back_out.at[part],
-            dst_ref=settled.at[pl.ds(levels * shards + starts[s], caps[s])],
+            src_ref=result[s] if full[s] else back_out.at[part],
+            dst_ref=back_in.at[part],
             send_sem=back_send.at[s],
             recv_sem=back_recv.at[s],
             device_id=partner,
             device_id_type=MESH,
         )
 
+    def other(k):
+        return lax.rem(me + k, shards)
+
+    def added(s, owner, theirs):
+        mine = grads[lookup(0, group, s, owner)].astype(jnp.float32)
+        summed[s, owner] = (mine + theirs.astype(jnp.float32)).astype(jnp.bfloat16)
+
+    def scatter_first():
+        for n in range(stride):
+            x_copy(n).wait_recv()
+            here = range(n * part, (n + 1) * part)
+            for i in here:
+                added(0, order[i], x_in[0][i])
+            for i in here:
+                owner = order[i]
+
+                @pl.when(owner != me)
+                def _():
+                    in_copy(0, owner, me).start()
+
+        gradient[0, me] = summed[0, me]
+
     def scatter(s):
-        x_copy(s).wait_recv()
-
-        @pl.loop(0, shards)
-        def _(o):
-            mine = grads[own_block[s, o]].astype(jnp.float32)
-            theirs = x_in[s][own_rank[s, o]].astype(jnp.float32)
-            summed[s, o] = (mine + theirs).astype(jnp.bfloat16)
+        x_copy(stride + s - 1).wait_recv()
+
+        if full[s]:
+            for i in range(shards):
+                added(s, order[i], x_in[s][i])
+        else:
+
+            @pl.loop(0, shards)
+            def _(o):
+                added(s, o, x_in[s][lookup(1, group, s, o)])
 
         gradient[s, me] = summed[s, me]
 
         @pl.loop(1, shards)
         def _(k):
-            in_copy(s, k).start()
+            in_copy(s, other(k), me).start()
 
     def compute(s):
         @pl.loop(1, shards)
         def _(k):
-            in_copy(s, k).wait_recv()
+            in_copy(s, me, other(k)).wait_recv()
 
         for copy in stat_copies(s):
             copy.wait()
@@ -238,21 +330,23 @@
 
         @pl.loop(1, shards)
         def _(k):
-            out_copy(s, k).start()
+            out_copy(s, other(k), me).start()
 
     def give_back(s):
         @pl.loop(1, shards)
         def _(k):
-            out_copy(s, k).wait_recv()
-
-        for i in range(caps[s]):
-            back_out[starts[s] + i] = result[s][pack_owner[s, i]]
+            out_copy(s, me, other(k)).wait_recv()
+
+        if not full[s]:
+            for i in range(caps[s]):
+                back_out[starts[s] + i] = result[s][lookup(3, group, s, i)]
         back_copy(s).start()
         for o in range(shards):
             settled[s * shards + o] = result[s][o]
 
-    ahead = min(2, levels)
-    for s in range(ahead):
+    ahead = min(AHEAD, levels)
+    scatter_first()
+    for s in range(1, ahead):
         scatter(s)
 
     @pl.loop(0, levels)
@@ -279,75 +373,48 @@
     give_back(levels - 1)
     for s in range(levels):
         back_copy(s).wait_recv()
-    for b in range(out.shape[0]):
-        out[b] = settled[pick[b]]
+        for i in range(caps[s]):
+            settled[levels * shards + starts[s] + i] = back_in[starts[s] + i]
     for s in range(levels):
 
         @pl.loop(1, shards)
         def _(k):
-            in_copy(s, k).wait_send()
-            out_copy(s, k).wait_send()
-
-        x_copy(s).wait_send()
+            in_copy(s, other(k), me).wait_send()
+            out_copy(s, other(k), me).wait_send()
+
         back_copy(s).wait_send()
-
-
-def pair_tables(owners, member, shards, levels, caps):
-    owner_of, slot_of, positions = slot_table(owners)
-    slots = jnp.arange(2 * levels, dtype=jnp.int32)
-    names = jnp.arange(shards, dtype=jnp.int32)
-    matches = (slot_of[None, None, :] == slots[:, None, None]) & (
-        owner_of[None, None, :] == names[None, :, None]
-    )
-    block = jnp.sum(jnp.where(matches, positions, 0), axis=2)
-    count = jnp.sum((owner_of[None, :] == names[:, None]).astype(jnp.int32), axis=1)
-    present = count[None, :] > slots[:, None]
-    before = names[None, :] < names[:, None]
-    rank = jnp.sum((present[:, None, :] & before[None]).astype(jnp.int32), axis=2)
-    rank = jnp.where(present, rank, 0)
-    places = jnp.arange(max(caps), dtype=jnp.int32)
-    at_place = present[:, None, :] & (rank[:, None, :] == places[None, :, None])
-    place_block = jnp.sum(jnp.where(at_place, block[:, None, :], 0), axis=2)
-    place_owner = jnp.sum(jnp.where(at_place, names, 0), axis=2)
-
-    def side(table, which):
-        return lax.dynamic_slice_in_dim(table, which * levels, levels, 0)
-
-    level = slot_of % levels
-    start = sum(jnp.where(level > s, caps[s], 0) for s in range(levels))
-    ahead_of = (count[None, :] > slot_of[:, None]) & (names[None, :] < owner_of[:, None])
-    block_rank = jnp.sum(ahead_of.astype(jnp.int32), axis=1)
-    pick = jnp.where(
-        slot_of // levels == member,
-        level * shards + owner_of,
-        levels * shards + start + block_rank,
-    )
-    return (
-        side(place_block, 1 - member),
-        side(block, member),
-        side(rank, member),
-        side(place_owner, member),
-        pick,
-    )
+    for n in range(len(parts)):
+        x_copy(n).wait_send()
+
+
+def settle_kernel(table, settled, out):
+    member = lax.axis_index("dp")
+    for b in range(out.shape[0]):
+        out[b] = settled[table[4 + member, b]]
 
 
 def pair_body(group_grads, owners, stats_left, stats_right):
     shards = lax.axis_size("fsdp")
-    member = lax.axis_index("dp")
     _, blocks, rows, width = group_grads.shape
     levels = stats_left.shape[1]
     caps = level_caps(blocks, shards, 2 * levels, levels)
-    tables = pair_tables(owners, member, shards, levels, caps)
     piece = (rows, width)
     dma = pltpu.SemaphoreType.DMA
     bf16 = jnp.bfloat16
     vmem = pl.BlockSpec(memory_space=pltpu.VMEM)
     smem = pl.BlockSpec(memory_space=pltpu.SMEM)
     anywhere = pl.BlockSpec(memory_space=pl.ANY)
-    return pl.pallas_call(
+    table = pl.pallas_call(
+        functools.partial(table_kernel, levels, shards, caps),
+        out_shape=jax.ShapeDtypeStruct((8, max(2 * levels * shards, blocks)), jnp.int32),
+        in_specs=[vmem],
+        out_specs=vmem,
+    )(owners.reshape(1, blocks))
+    messages = visit_order(shards)[0] + levels - 1
+    settled = pl.pallas_call(
         functools.partial(fused_kernel, caps),
-        out_shape=jax.ShapeDtypeStruct((blocks, *piece), bf16),
-        in_specs=[smem] * 5 + [vmem, anywhere, anywhere],
+        out_shape=jax.ShapeDtypeStruct((levels * shards + sum(caps), *piece), bf16),
+        in_specs=[smem, vmem, anywhere, anywhere],
         out_specs=vmem,
         scratch_shapes=[
             pltpu.VMEM((levels, width, width), jnp.float32),
@@ -356,11 +423,10 @@
             pltpu.VMEM((levels, shards, *piece), bf16),
             pltpu.VMEM((levels, shards, *piece), bf16),
             pltpu.VMEM((levels, shards, *piece), bf16),
-            pltpu.VMEM((levels * shards + sum(caps), *piece), bf16),
             pltpu.VMEM((sum(caps), *piece), bf16),
             dma((2, levels)),
-            dma((levels,)),
-            dma((levels,)),
+            dma((messages,)),
+            dma((messages,)),
             dma((levels, shards)),
             dma((levels, shards)),
             dma((levels, shards)),
@@ -369,11 +435,19 @@
             dma((levels,)),
         ]
         + [pltpu.VMEM((cap, *piece), bf16) for cap in caps]
-        + [pltpu.VMEM((shards, *piece), bf16)] * levels,
+        + [pltpu.VMEM((shards, *piece), bf16)] * levels
+        + [pltpu.VMEM((sum(caps), *piece), bf16)],
         compiler_params=pltpu.CompilerParams(
-            collective_id=0, has_side_effects=True, vmem_limit_bytes=56 * 1024 * 1024
+            collective_id=0, has_side_effects=True, vmem_limit_bytes=48 * 1024 * 1024
         ),
-    )(*tables, group_grads[0], stats_left[0], stats_right[0])
+    )(table, group_grads[0], stats_left[0], stats_right[0])
+    return pl.pallas_call(
+        settle_kernel,
+        out_shape=jax.ShapeDtypeStruct((blocks, *piece), bf16),
+        in_specs=[smem, vmem],
+        out_specs=vmem,
+        compiler_params=pltpu.CompilerParams(vmem_limit_bytes=16 * 1024 * 1024),
+    )(table, settled)
 
 
 def body(group_grads, owners, stats_left, stats_right):

time: 135 us -> 135 us (level)
  the two profiles are of different devices: /device:TPU:22 before, /device:TPU:31 now
where the time goes in v2:
time: 135 us
  Pallas kernels  133 us (99%)
  local copies, waits for them, and re-layouts  2.07 us (2%)
    pallas_call x1, Pallas kernels, pair_body(): pl.pallas_call(functools.partial(fused_kernel, caps), out_shape=jax.Shape...  129 us

profile of v2, /device:TPU:31, one launch (start us, length us, event | category | flops | bytes accessed | tf_op | source)
XLA Modules:
  0.0 134.6 jit_solution(11252544794213675922)
XLA Ops:
  0.0 1.5 %shard_map.46.table = s32[8,128]{1,0:T(8,128)} custom-call(s32[1,46]{1,0:T(1,128)} %bitcast.7), custom_call_target="tpu_custom_call" | custom-call | tf_op jit(solution)/shard_map/pallas_call | solution.py:407
  1.5 0.0 copy-start
  1.5 1.4 %copy-done = bf16[1,46,32,512]{3,2,1,0:T(8,128)(2,1)S(1)} copy-done((bf16[1,46,32,512]{3,2,1,0:T(8,128)(2,1)S(1)}, bf16[1,46,32,512]{3,2,1,0:T(8,128)(2,1)}, u32[]{:S(2)}) %copy-start) | copy-done | bytes 1507352
  2.9 0.0 copy-start.1
  2.9 0.7 copy-done.1
  3.6 129.2 %shard_map.47.settled = bf16[116,32,512]{2,1,0:T(8,128)(2,1)S(1)} custom-call(s32[8,128]{1,0:T(8,128)S(1)} %copy-done.1, bf16[46,32,512]{2,1,0:T(8,128)(2,1)S(1)} %bitcast.4, f32[4,512,512]{2,1,0:T(8,128)} %bitcast.5, f32[4,512,512]{2,1,0:T(8,128)} %bitcast.6), custom_call_target="tpu_custom_call" | custom-call | tf_op jit(solution)/shard_map/pallas_call | solution.py:414
  132.8 1.8 %shard_map.48 = bf16[46,32,512]{2,1,0:T(8,128)(2,1)} custom-call(s32[8,128]{1,0:T(8,128)S(1)} %copy-done.1, bf16[116,32,512]{2,1,0:T(8,128)(2,1)S(1)} %shard_map.47.settled), custom_call_target="tpu_custom_call" | custom-call | tf_op jit(solution)/shard_map/pallas_call | solution.py:444
Async XLA Ops:
  1.5 1.4 %copy-start = (bf16[1,46,32,512]{3,2,1,0:T(8,128)(2,1)S(1)}, bf16[1,46,32,512]{3,2,1,0:T(8,128)(2,1)}, u32[]{:S(2)}) copy-start(bf16[1,46,32,512]{3,2,1,0:T(8,128)(2,1)} %param.4) | copy-start | bytes 4521988
  2.9 0.7 copy-start.1
